TPU v7x, 16 devices: a whole 2x2x2 slice. The times are simulated.
16 devices in a mesh: row: 2 (over z), col: 8 (over y, x, core).
Axes of the slice: x: 2, y: 2, z: 2, core: 2. Of those that a mesh axis runs over, the one named last changes fastest.
Arguments:
- v_panels: float32 [8192, 8192], P('row', 'col')
- t_factors: float32 [64, 128, 128], P('col')
- z_vectors: float32 [8192, 4096], P(None, ('col', 'row'))
Outputs:
- output: float32 [8192, 4096], P('row', 'col')
All inputs are finite; a program needn't handle non-finite values.
Results may differ from a plain program's by a relative error of at most 0.001.
Values sent between devices are 32-bit elements.
A program may use at most 1 GiB of HBM per device.

v0:
```python
import jax
import jax.numpy as jnp
from jax import lax
from jax.sharding import PartitionSpec as P

FULL_PRECISION = lax.Precision.HIGHEST


def solution(mesh):
    def local_program(v_local, t_local, z_local):
        x_start = lax.all_to_all(z_local, "row", 0, 1, tiled=True)
        v_rows = lax.all_gather(v_local, "col", axis=1, tiled=True)
        t_all = lax.all_gather(t_local, "col", axis=0, tiled=True)
        panel_count = t_all.shape[0]
        width = t_all.shape[1]

        def apply_panel(step, x_cur):
            panel_idx = panel_count - 1 - step
            v_pan = lax.dynamic_slice_in_dim(v_rows, panel_idx * width, width, axis=1)
            t_pan = lax.dynamic_index_in_dim(t_all, panel_idx, axis=0, keepdims=False)
            w_part = lax.dot_general(v_pan, x_cur, (((0,), (0,)), ((), ())), precision=FULL_PRECISION, preferred_element_type=jnp.float32)
            w_full = lax.psum(w_part, "row")
            y_mat = jnp.dot(t_pan, w_full, precision=FULL_PRECISION, preferred_element_type=jnp.float32)
            return x_cur - jnp.dot(v_pan, y_mat, precision=FULL_PRECISION, preferred_element_type=jnp.float32)

        return lax.fori_loop(0, panel_count, apply_panel, x_start)

    return jax.shard_map(local_program, mesh=mesh, in_specs=(P("row", "col"), P("col", None, None), P(None, ("col", "row"))), out_specs=P("row", "col"), check_vma=False)
```

profile of v0, /device:TPU:7, one launch (start us, length us, event | category | flops | bytes accessed | tf_op | source)
XLA Modules:
  0.0 3348.0 jit_solution(12356787053027118989)
XLA Ops:
  15.0 91.5 %all-to-all-done = f32[2,4096,256]{2,1,0:T(8,128)} async-done(((f32[2,4096,256]{2,1,0:T(8,128)}), f32[2,4096,256]{2,1,0:T(8,128)}, u32[]{:S(2)}, u32[]{:S(2)}) %all-to-all-start) | async-done | bytes 8388640 | tf_op jit(solution)/shard_map/all_to_all | solution.py:11
  124.4 502.8 %all-gather.3.cloned.1.call-done = f32[4096,8192]{1,0:T(8,128)} async-done(((f32[4096,1024]{1,0:T(8,128)}), f32[4096,8192]{1,0:T(8,128)}) %all-gather.3.cloned.1.call-update) | async-done | bytes 134217744 | tf_op jit(solution)/shard_map/all_gather | solution.py:12
  627.2 2714.3 %while.15 = (s32[]{:T(128)}, f32[4096,512]{1,0:T(8,128)}, f32[4096,8192]{1,0:T(8,128)}, f32[64,128,128]{2,1,0:T(8,128)}, s32[]{:T(128)}, /*index=5*/s32[]{:T(128)}, s32[]{:T(128)}, s32[]{:T(128)}, s32[]{:T(128)}, s32[]{:T(128)}) while((s32[]{:T(128)}, f32[4096,512]{1,0:T(8,128)}, f32[4096,8192]{1,0:T(8,128)}, f32[64,128,128]{2,1,0:T(8,128)}, ...), condition=%wide.region_2.3_spmd, body=%wide.region_0.2_spmd.sunk | while | flops 6545276928 | bytes 32047356 | solution.py:26
  637.0 19.6 all-reduce.2.cloned.1.call-done
  679.6 19.4 all-reduce.2.cloned.1.call-done
  722.0 19.4 all-reduce.2.cloned.1.call-done
  1188.5 19.4 all-reduce.2.cloned.1.call-done
  1230.9 19.4 all-reduce.2.cloned.1.call-done
  1273.3 19.4 all-reduce.2.cloned.1.call-done
  1315.7 19.4 all-reduce.2.cloned.1.call-done
  1358.1 19.4 all-reduce.2.cloned.1.call-done
  1400.5 19.4 all-reduce.2.cloned.1.call-done
  1443.0 19.4 all-reduce.2.cloned.1.call-done
  1485.4 19.4 all-reduce.2.cloned.1.call-done
  1527.8 19.4 all-reduce.2.cloned.1.call-done
  1994.3 19.4 all-reduce.2.cloned.1.call-done
  2036.7 19.4 all-reduce.2.cloned.1.call-done
  2079.1 19.4 all-reduce.2.cloned.1.call-done
  2121.5 19.4 all-reduce.2.cloned.1.call-done
  2163.9 19.4 all-reduce.2.cloned.1.call-done
  2206.3 19.4 all-reduce.2.cloned.1.call-done
  2248.7 19.4 all-reduce.2.cloned.1.call-done
  2291.1 19.4 all-reduce.2.cloned.1.call-done
  2333.5 19.4 all-reduce.2.cloned.1.call-done
  (371 shorter events, 2330.4 us)
Async XLA Ops:
  6.5 117.8 %all-gather.5.cloned.1.call-start = ((), (), s32[]{:S(2)}) async-start(), calls=%async_computation.2 | async-start | bytes 4718592 | tf_op jit(solution)/shard_map/all_gather | solution.py:13
  7.3 619.9 %all-gather.3.cloned.1.call-start = ((), (), s32[]{:S(2)}) async-start(), calls=%async_computation.1 | async-start | bytes 150994944 | tf_op jit(solution)/shard_map/all_gather | solution.py:12
  8.0 98.5 %all-to-all-start = ((f32[2,4096,256]{2,1,0:T(8,128)}), f32[2,4096,256]{2,1,0:T(8,128)}, u32[]{:S(2)}, u32[]{:S(2)}) async-start(f32[2,4096,256]{2,1,0:T(8,128)} %bitcast.19), calls=%async_computation | async-start | bytes 16777216 | tf_op jit(solution)/shard_map/all_to_all | solution.py:11
  627.2 29.4 all-reduce.2.cloned.1.call-start
  669.8 29.3 all-reduce.2.cloned.1.call-start
  712.2 29.3 all-reduce.2.cloned.1.call-start
  754.6 29.3 all-reduce.2.cloned.1.call-start
  797.0 29.3 all-reduce.2.cloned.1.call-start
  1178.7 29.3 all-reduce.2.cloned.1.call-start
  1221.1 29.3 all-reduce.2.cloned.1.call-start
  1263.5 29.3 all-reduce.2.cloned.1.call-start
  1305.9 29.3 all-reduce.2.cloned.1.call-start
  1348.3 29.3 all-reduce.2.cloned.1.call-start
  1390.7 29.3 all-reduce.2.cloned.1.call-start
  1433.1 29.3 all-reduce.2.cloned.1.call-start
  1475.5 29.3 all-reduce.2.cloned.1.call-start
  1517.9 29.3 all-reduce.2.cloned.1.call-start
  1560.3 29.3 all-reduce.2.cloned.1.call-start
  1602.8 29.3 all-reduce.2.cloned.1.call-start
  1984.4 29.3 all-reduce.2.cloned.1.call-start
  2026.8 29.3 all-reduce.2.cloned.1.call-start
  2069.2 29.3 all-reduce.2.cloned.1.call-start
  2111.7 29.3 all-reduce.2.cloned.1.call-start
  2154.1 29.3 all-reduce.2.cloned.1.call-start
  (43 other events, 1258.7 us)
Sparse Core Ops, SparseCore 0:
  9.2 33.0 all-gather.4
  44.2 582.9 all-gather.2
  637.1 19.4 all-reduce.1
  679.7 19.2 all-reduce.1
  722.1 19.2 all-reduce.1
  764.5 19.2 all-reduce.1
  806.9 19.2 all-reduce.1
  849.3 19.2 all-reduce.1
  891.8 19.2 all-reduce.1
  934.2 19.2 all-reduce.1
  976.6 19.2 all-reduce.1
  1019.0 19.2 all-reduce.1
  1061.4 19.2 all-reduce.1
  1103.8 19.2 all-reduce.1
  1146.2 19.2 all-reduce.1
  1188.6 19.2 all-reduce.1
  1231.0 19.2 all-reduce.1
  1273.4 19.2 all-reduce.1
  1315.8 19.2 all-reduce.1
  1358.2 19.2 all-reduce.1
  1400.7 19.2 all-reduce.1
  1443.1 19.2 all-reduce.1
  1485.5 19.2 all-reduce.1
  1527.9 19.2 all-reduce.1
  (42 shorter events, 807.7 us)
where the time goes:
time: 3350 us
  waiting for transfers between devices  1840 us (55%)
  matrix products  1470 us (44%)
    psum x64, waiting for transfers between devices, apply_panel(): w_full = lax.psum(w_part, 'row')  1240 us
    dot_general x64, matrix products, apply_panel(): jnp.dot(v_pan, y_mat, precision=FULL_PRECISION, preferred_element_type=jn...  753 us
    dot_general x64, matrix products, apply_panel(): lax.dot_general(v_pan, x_cur, (((0,), (0,)), ((), ())), precision=FULL_PR...  627 us
    all_gather x1, waiting for transfers between devices, local_program(): v_rows = lax.all_gather(v_local, 'col', axis=1, tiled=True)  503 us
    all_to_all x1, waiting for transfers between devices, local_program(): x_start = lax.all_to_all(z_local, 'row', 0, 1, tiled=True)  91.5 us
    dot_general x64, matrix products, apply_panel(): jnp.dot(t_pan, w_full, precision=FULL_PRECISION, preferred_element_type=j...  86.7 us
  transfers between devices with their start and end apart: 67, of which 66 were waited for; matrix products, arithmetic and copies ran while one was open for 1% of the time, Pallas kernels for 0%

commit v1 on v0

v1 whole, which is shorter than its diff:
```python
import functools

import jax
import jax.numpy as jnp
from jax import lax
from jax.experimental import pallas as pl
from jax.experimental.pallas import tpu as pltpu
from jax.sharding import PartitionSpec as P

HI = lax.Precision.HIGHEST
MESH = pl.DeviceIdType.MESH
NCH = 32
NU = NCH // 2
NT = NU * (NU + 1)
HOP = 5
PRE = 2
LATE = 5 * HOP + 2
LAG = LATE + PRE
RING = 32
LRING = 4
FIRST = NCH - 2


def dot(a, b):
    return jnp.dot(a, b, precision=HI, preferred_element_type=jnp.float32)


def dot_t(a, b):
    return lax.dot_general(a, b, (((0,), (0,)), ((), ())), precision=HI, preferred_element_type=jnp.float32)


def unit_of(i, t):
    half = NU // 2
    top = (NCH - 1 - i) // 2
    inner = jnp.where(lax.rem(t, 2) == 0, top + t // 2, half + t // 2)
    return jnp.where(t < 2 * (half - top), inner, top + t)


def split(v):
    high = v.astype(jnp.bfloat16)
    rest = v - high.astype(jnp.float32)
    mid = rest.astype(jnp.bfloat16)
    low = (rest - mid.astype(jnp.float32)).astype(jnp.bfloat16)
    return high, mid, low


def product(a, b):
    def d(p, q):
        return jnp.dot(a[p], b[q], preferred_element_type=jnp.float32)
    return ((d(2, 0) + d(0, 2) + d(1, 1)) + (d(1, 0) + d(0, 1))) + d(0, 0)


def kernel(ts, v_ref, t_ref, z_ref, out_ref, vb_ref, tb_ref, xs, vv, ws, gs, yp, tv, stage, xr, ystage, yr,
           recv, recv_t, snd, snd_t, lsem, tsem, zsem, osem, xsend, xrecv, ysend, yrecv):
    hb = ts // 2
    us = 2 * ts
    z = lax.axis_index("row")
    col = lax.axis_index("col")
    core = lax.rem(col, 2)
    x = lax.rem(col // 2, 2)
    y = col // 4
    half = NU // 2

    def flip(q):
        nx = jnp.where(q == 0, 1 - x, x)
        ny = jnp.where(q == 1, 1 - y, y)
        nz = jnp.where(q == 2, 1 - z, z)
        return (nz, (ny * 2 + nx) * 2 + core)

    sibling = (z, col + 1 - 2 * core)

    zcopy = pltpu.make_async_copy(z_ref, xs, zsem)
    zcopy.start()
    barrier = pltpu.get_barrier_semaphore()
    for d in [flip(0), flip(1), flip(2), sibling]:
        pl.semaphore_signal(barrier, inc=1, device_id=d, device_id_type=MESH)
    pl.semaphore_wait(barrier, 4)

    def role(n, i, t):
        g = NCH - 1 - i
        ro = unit_of(i, t) // half
        co = g // 4
        ax = lax.rem(x + lax.rem(co // 2, 2), 2)
        ay = lax.rem(y + co // 4, 2)
        az = lax.rem(z + ro, 2)
        k = lax.rem(n, 3)
        a = jnp.where(k == 0, ax, jnp.where(k == 1, ay, az))
        b = jnp.where(k == 0, ay, jnp.where(k == 1, az, ax))
        c = jnp.where(k == 0, az, jnp.where(k == 1, ax, ay))
        s = a + b + c
        off = lax.rem(co + core, 2)
        depth = jnp.where(a == 1, s, jnp.where(s == 0, 0, 2 + s)) + off
        return k, a, b, c, s, off, depth

    def v_src(i, t, lane, size):
        g = NCH - 1 - i
        first = lax.rem(unit_of(i, t), half) * us + lane * ts
        return v_ref.at[pl.ds(pl.multiple_of(first, ts), size), pl.ds(pl.multiple_of(lax.rem(g, 4) * ts, ts), ts)]

    def short(i, t):
        return jnp.logical_and(t == 0, lax.rem(i, 2) == 0)

    def ship(root, n, i, t, lane, kind, to, dev):
        g = NCH - 1 - i
        there = vb_ref.at[n, pl.ds(pl.multiple_of(lane * ts, ts), ts)]
        t_there = tb_ref.at[i, lane]
        cv = pltpu.make_async_remote_copy(
            src_ref=v_src(i, t, lane, ts) if root else there, dst_ref=there,
            send_sem=snd.at[kind, lax.rem(n, RING)], recv_sem=recv.at[to, n], device_id=dev, device_id_type=MESH)
        ct = pltpu.make_async_remote_copy(
            src_ref=t_ref.at[lax.rem(g, 4) * 2 + lane] if root else t_there, dst_ref=t_there,
            send_sem=snd_t.at[kind, i], recv_sem=recv_t.at[to, i], device_id=dev, device_id_type=MESH)
        return cv, ct

    def both(i, t, lane, do_v, do_t):
        pl.when(jnp.logical_not(jnp.logical_and(short(i, t), lane == 0)))(do_v)
        pl.when(t == 0)(do_t)

    def start(root, n, i, t, lane, kind, to, dev):
        cv, ct = ship(root, n, i, t, lane, kind, to, dev)
        both(i, t, lane, cv.start, ct.start)

    def arrived(n, i, t, lane, to):
        cv, ct = ship(False, n, i, t, lane, 0, to, sibling)
        both(i, t, lane, cv.wait_recv, ct.wait_recv)

    def sent(n, i, t, lane, kind):
        cv, ct = ship(False, n, i, t, lane, kind, 0, sibling)
        both(i, t, lane, cv.wait_send, ct.wait_send)

    def slot(tau, st):
        st = list(st)
        for d in range(7):
            i, t = st[2 * d], st[2 * d + 1]
            n = tau - (d * HOP if d < 6 else LATE)
            live = jnp.logical_and(n >= 0, n < NT)
            k, a, b, c, s, off, depth = role(n, i, t)
            if d < 6:
                @pl.when(jnp.logical_and(live, depth == d))
                def _():
                    root = d == 0
                    if root:
                        start(root, n, i, t, core, 0, 0, flip(k))
                        start(root, n, i, t, 1 - core, 4, 0, sibling)
                        start(root, n, i, t, core, 3, 1, sibling)
                        return
                    arrived(n, i, t, core, 0)
                    if d < 5:
                        @pl.when(jnp.logical_or(s == 0, jnp.logical_and(a == 1, s >= 2)))
                        def _():
                            start(root, n, i, t, core, 0, 0, flip(k))
                    if d < 3:
                        @pl.when(jnp.logical_and(a == 1, s == 1))
                        def _():
                            start(root, n, i, t, core, 1, 0, flip(lax.rem(k + 1, 3)))
                    if d < 4:
                        @pl.when(jnp.logical_and(a == 1, c == 0))
                        def _():
                            start(root, n, i, t, core, 2, 0, flip(lax.rem(k + 2, 3)))

                    @pl.when(s > 0)
                    def _():
                        start(root, n, i, t, core, 3, 1, sibling)
            else:
                @pl.when(live)
                def _():
                    owner = s + off == 0

                    @pl.when(jnp.logical_not(owner))
                    def _():
                        arrived(n, i, t, 1 - core, 1)

                    @pl.when(jnp.logical_or(s > 0, off == 0))
                    def _():
                        sent(n, i, t, core, 3)

                    @pl.when(owner)
                    def _():
                        sent(n, i, t, 1 - core, 4)

                    @pl.when(jnp.logical_or(s == 0, jnp.logical_and(a == 1, s >= 2)))
                    def _():
                        sent(n, i, t, core, 0)

                    @pl.when(jnp.logical_and(a == 1, s == 1))
                    def _():
                        sent(n, i, t, core, 1)

                    @pl.when(jnp.logical_and(a == 1, c == 0))
                    def _():
                        sent(n, i, t, core, 2)
            end = t + 1 > i // 2
            st[2 * d] = jnp.where(n >= 0, jnp.where(end, i + 1, i), i)
            st[2 * d + 1] = jnp.where(n >= 0, jnp.where(end, 0, t + 1), t)
        return tuple(st)

    def is_owner(i, t):
        g = NCH - 1 - i
        return jnp.logical_and(g // 4 == col, unit_of(i, t) // half == z)

    def first_of(i):
        a = i // 2
        return a * (a + 1) + lax.rem(i, 2) * (a + 1)

    def load_or_wait(i, t, go):
        n = first_of(i) + t
        u = unit_of(i, t)
        sem = lsem.at[lax.rem(n, LRING)]

        def piece(own, skip):
            src = v_src(i, t, skip // ts, us - skip) if own else vb_ref.at[n, pl.ds(skip, us - skip)]
            dst = vv.at[lax.rem(i, 2), pl.ds(pl.multiple_of(u * us + skip, ts), us - skip)]
            return pltpu.make_async_copy(src, dst, sem)

        if not go:
            pl.when(short(i, t))(lambda: piece(False, ts).wait())
            pl.when(jnp.logical_not(short(i, t)))(lambda: piece(False, 0).wait())
            return
        own = is_owner(i, t)
        for o in (True, False):
            for skip in (0, ts):
                here = own if o else jnp.logical_not(own)
                part = short(i, t) if skip else jnp.logical_not(short(i, t))

                @pl.when(jnp.logical_and(here, part))
                def _():
                    piece(o, skip).start()

    def load(i, t):
        load_or_wait(i, t, True)

    def loaded(i, t):
        load_or_wait(i, t, False)

    def load_t(i):
        g = NCH - 1 - i
        own = is_owner(i, 0)
        sem = tsem.at[lax.rem(i, 2)]

        @pl.when(own)
        def _():
            pltpu.make_async_copy(t_ref.at[pl.ds(lax.rem(g, 4) * 2, 2)], tv.at[lax.rem(i, 2)], sem).start()

        @pl.when(jnp.logical_not(own))
        def _():
            pltpu.make_async_copy(tb_ref.at[i], tv.at[lax.rem(i, 2)], sem).start()

    def loaded_t(i):
        pltpu.make_async_copy(tb_ref.at[i], tv.at[lax.rem(i, 2)], tsem.at[lax.rem(i, 2)]).wait()

    def rows(u):
        return pl.ds(pl.multiple_of(u * us, us), us)

    other = (1 - z, col)

    def cross(q):
        return pltpu.make_async_remote_copy(
            src_ref=stage.at[rows(q)], dst_ref=xr.at[rows(q)], send_sem=xsend.at[q], recv_sem=xrecv.at[q],
            device_id=other, device_id_type=MESH)

    def cross_y(j):
        return pltpu.make_async_remote_copy(
            src_ref=ystage.at[j], dst_ref=yr.at[j], send_sem=ysend.at[j], recv_sem=yrecv.at[j],
            device_id=other, device_id_type=MESH)

    zero = jnp.int32(0)
    st = (zero,) * 14
    yp[...] = jnp.zeros_like(yp)

    def clear(q, carry):
        for p in range(2):
            vv[p, rows(q), :] = jnp.zeros((us, ts), jnp.float32)
        return carry

    lax.fori_loop(0, NU, clear, 0)
    st = lax.fori_loop(0, LAG, slot, st)
    zcopy.wait()
    load(zero, zero)

    def chunk(i, st):
        top = (NCH - 1 - i) // 2
        count = i // 2 + 1
        now = lax.rem(i, 2)
        old = 1 - now
        base = first_of(i)
        leaving = i == FIRST
        load_t(i)

        def prepare(t, st):
            st = slot(base + t + LAG, st)

            @pl.when(t + PRE < count)
            def _():
                load(i, t + PRE)
            return st

        def update(u):
            y = [yp[p] for p in range(3)]
            xs[rows(u), :] = xs[rows(u), :] - product(split(vv[old, rows(u), :]), y)

        def gather(u):
            v = vv[now, rows(u), :]
            return dot_t(v, xs[rows(u), :]), dot_t(v[:, :ts // 2], v[:, ts // 2:])

        def leave(u):
            @pl.when(jnp.logical_and(leaving, u // half == 1 - z))
            def _():
                stage[rows(lax.rem(u, half)), :] = xs[rows(u), :]

        def go(u):
            @pl.when(jnp.logical_and(leaving, u // half == 1 - z))
            def _():
                cross(lax.rem(u, half)).start()

        st = prepare(zero, st)
        update(top)
        leave(top)
        ws[...] = jnp.zeros_like(ws)
        gs[...] = jnp.zeros_like(gs)

        @pl.when(i == FIRST + 1)
        def _():
            cross_y(0).start()

        def unit(t, st):
            st = prepare(t, st)
            loaded(i, t - 1)
            u, v = unit_of(i, t - 1), unit_of(i, t)
            w, gg = gather(u)
            update(v)
            ws[...] += w
            gs[...] += gg
            leave(v)
            go(u)
            return st

        st = lax.fori_loop(1, count, unit, st)
        loaded(i, count - 1)
        w, gg = gather(unit_of(i, count - 1))
        ws[...] += w
        gs[...] += gg
        go(unit_of(i, count - 1))
        for p in range(PRE):
            @pl.when(jnp.logical_and(i + 1 < NCH, p < (i + 1) // 2 + 1))
            def _():
                load(i + 1, jnp.int32(p))
        loaded_t(i)
        y2 = dot(tv[now, 1], ws[hb:, :])
        y1 = dot(tv[now, 0], ws[:hb, :] - dot(gs[...], y2))
        for p, q in enumerate(split(y1)):
            yp[p, :hb, :] = q
        for p, q in enumerate(split(y2)):
            yp[p, hb:, :] = q

        @pl.when(i >= FIRST)
        def _():
            ystage[i - FIRST, :hb, :] = y1
            ystage[i - FIRST, hb:, :] = y2
        return st

    lax.fori_loop(0, NCH, chunk, st)

    def place(src, q, row, sem):
        return pltpu.make_async_copy(
            src, out_ref.at[rows(q), pl.ds(pl.multiple_of(row * ts, ts), ts)], sem)

    def mine(q):
        return place(xs.at[rows(half * z + q)], q, z, osem.at[q])

    def theirs(q):
        return place(xr.at[rows(q)], q, 1 - z, osem.at[half + q])

    def last(q, carry):
        y = [yp[p] for p in range(3)]
        r = rows(half * z + q)
        xs[r, :] = xs[r, :] - product(split(vv[(NCH - 1) % 2, r, :]), y)

        @pl.when(q == 0)
        def _():
            cross_y(1).start()

        @pl.when(q > 0)
        def _():
            mine(q - 1).start()
        return carry

    lax.fori_loop(0, half, last, 0)

    for j in range(2):
        cross_y(j).wait_recv()

    def last_theirs(q, carry):
        r = rows(half * z + q)
        cross(q).wait_recv()
        before = xr[rows(q), :] - dot(vv[FIRST % 2, r, :], yr[0])
        xr[rows(q), :] = before - dot(vv[1 - FIRST % 2, r, :], yr[1])

        @pl.when(q == 0)
        def _():
            mine(half - 1).start()

        @pl.when(q > 0)
        def _():
            theirs(q - 1).start()
        return carry

    lax.fori_loop(0, half, last_theirs, 0)
    for j in range(2):
        cross_y(j).wait_send()

    def drain(q, carry):
        mine(q).wait()
        cross(q).wait_send()
        return carry

    lax.fori_loop(0, half, drain, 0)
    theirs(half - 1).start()

    def drain_theirs(q, carry):
        theirs(q).wait()
        return carry

    lax.fori_loop(0, half, drain_theirs, 0)


def solution(mesh):
    def local_program(v_local, t_local, z_local):
        n = z_local.shape[0]
        ts = n // NCH
        f32 = jnp.float32
        any_ = pl.BlockSpec(memory_space=pl.ANY)
        dma = pltpu.SemaphoreType.DMA
        out, _, _ = pl.pallas_call(
            functools.partial(kernel, ts),
            out_shape=(jax.ShapeDtypeStruct((n // 2, 2 * ts), f32),
                       jax.ShapeDtypeStruct((NT, 2 * ts, ts), f32),
                       jax.ShapeDtypeStruct((NCH, 2, ts // 2, ts // 2), f32)),
            in_specs=[any_] * 3,
            out_specs=(any_,) * 3,
            scratch_shapes=[
                pltpu.VMEM((n, ts), f32),
                pltpu.VMEM((2, n, ts), f32),
                pltpu.VMEM((ts, ts), f32),
                pltpu.VMEM((ts // 2, ts // 2), f32),
                pltpu.VMEM((3, ts, ts), jnp.bfloat16),
                pltpu.VMEM((2, 2, ts // 2, ts // 2), f32),
                pltpu.VMEM((n // 2, ts), f32),
                pltpu.VMEM((n // 2, ts), f32),
                pltpu.VMEM((2, ts, ts), f32),
                pltpu.VMEM((2, ts, ts), f32),
                dma((2, NT)), dma((2, NCH)), dma((5, RING)), dma((5, NCH)),
                dma((LRING,)), dma((2,)), dma, dma((NU,)),
                dma((NU // 2,)), dma((NU // 2,)), dma((2,)), dma((2,)),
            ],
            compiler_params=pltpu.CompilerParams(collective_id=0, has_side_effects=True, vmem_limit_bytes=60 * 1024 * 1024),
            name="back_transform",
        )(v_local, t_local, z_local)
        return out

    return jax.shard_map(local_program, mesh=mesh, in_specs=(P("row", "col"), P("col", None, None), P(None, ("col", "row"))),
                         out_specs=P("row", "col"), check_vma=False)
```

time: 3350 us -> 792 us (0.24)
  waiting for transfers between devices: 1840 us -> 0 us
  matrix products: 1470 us -> 0 us
  Pallas kernels: 0 us -> 785 us
    dot_general x192 -> x0, matrix products: 1470 us -> none  [the longest x64 753 us: apply_panel(): jnp.dot(v_pan, y_mat, precision=FULL_PRECISION, preferred_element_type=jn...]
    psum x64 -> x0, waiting for transfers between devices: 1240 us -> none  [apply_panel(): w_full = lax.psum(w_part, 'row')]
    pallas_call x0 -> x1, Pallas kernels: none -> 785 us  [local_program(): pl.pallas_call(functools.partial(kernel, ts), out_shape=(jax.ShapeDtypeSt...]
    all_gather x2 -> x0, waiting for transfers between devices: 503 us -> none  [the longest x1 503 us: local_program(): v_rows = lax.all_gather(v_local, 'col', axis=1, tiled=True)]
    all_to_all x1 -> x0, waiting for transfers between devices: 91.5 us -> none  [local_program(): x_start = lax.all_to_all(z_local, 'row', 0, 1, tiled=True)]
  transfers between devices with their start and end apart: 67 -> 0, of which waited for: 66 -> 0; matrix products, arithmetic and copies ran while one was open for 1% -> 0% of each run, Pallas kernels for 0% -> 0%
where the time goes in v1:
time: 792 us
  Pallas kernels  785 us (99%)
    pallas_call x1, Pallas kernels, local_program(): pl.pallas_call(functools.partial(kernel, ts), out_shape=(jax.ShapeDtypeSt...  785 us

profile of v1, /device:TPU:7, one launch (start us, length us, event | category | flops | bytes accessed | tf_op | source)
XLA Modules:
  0.0 792.4 jit_solution(1330450602250552635)
XLA Ops:
  0.0 784.6 %back_transform.1 = (f32[4096,512]{1,0:T(8,128)}, f32[272,512,256]{2,1,0:T(8,128)}, f32[32,2,128,128]{3,2,1,0:T(8,128)}) custom-call(f32[4096,1024]{1,0:T(8,128)} %v_ref.1, f32[8,128,128]{2,1,0:T(8,128)} %t_ref.1, f32[8192,256]{1,0:T(8,128)} %z_ref.1), custom_call_target="tpu_custom_call" | custom-call | tf_op jit(solution)/shard_map/back_transform/pallas_call | solution.py:433
  784.6 7.8 copy.5

commit v2 on v1

--- a/solution.py
+++ b/solution.py
@@ -12,12 +12,13 @@
 NCH = 32
 NU = NCH // 2
 NT = NU * (NU + 1)
-HOP = 5
+HOP = 6
 PRE = 2
 LATE = 5 * HOP + 2
 LAG = LATE + PRE
-RING = 32
+RING = 64
 LRING = 4
+EARLY = 5
 FIRST = NCH - 2
 
 
@@ -308,9 +309,11 @@
                 stage[rows(lax.rem(u, half)), :] = xs[rows(u), :]
 
         def go(u):
-            @pl.when(jnp.logical_and(leaving, u // half == 1 - z))
+            q = lax.rem(u, half)
+
+            @pl.when(jnp.logical_and(leaving, jnp.logical_and(u // half == 1 - z, q < EARLY)))
             def _():
-                cross(lax.rem(u, half)).start()
+                cross(q).start()
 
         st = prepare(zero, st)
         update(top)
@@ -378,6 +381,8 @@
         @pl.when(q == 0)
         def _():
             cross_y(1).start()
+            for p in range(EARLY, half):
+                cross(p).start()
 
         @pl.when(q > 0)
         def _():

time: 792 us -> 784 us (0.990)
  Pallas kernels: 785 us -> 776 us
    pallas_call x1, Pallas kernels: 785 us -> 776 us  [local_program(): pl.pallas_call(functools.partial(kernel, ts), out_shape=(jax.ShapeDtypeSt...]
where the time goes in v2:
time: 784 us
  Pallas kernels  776 us (99%)
    pallas_call x1, Pallas kernels, local_program(): pl.pallas_call(functools.partial(kernel, ts), out_shape=(jax.ShapeDtypeSt...  776 us

profile of v2, /device:TPU:7, one launch (start us, length us, event | category | flops | bytes accessed | tf_op | source)
XLA Modules:
  0.0 783.8 jit_solution(10217468974623070729)
XLA Ops:
  0.0 776.0 %back_transform.1 = (f32[4096,512]{1,0:T(8,128)}, f32[272,512,256]{2,1,0:T(8,128)}, f32[32,2,128,128]{3,2,1,0:T(8,128)}) custom-call(f32[4096,1024]{1,0:T(8,128)} %v_ref.1, f32[8,128,128]{2,1,0:T(8,128)} %t_ref.1, f32[8192,256]{1,0:T(8,128)} %z_ref.1), custom_call_target="tpu_custom_call" | custom-call | tf_op jit(solution)/shard_map/back_transform/pallas_call | solution.py:438
  776.0 7.8 copy.5
